TPU v7x, 32 devices: a whole 2x2x4 slice. The times are simulated.
32 devices in a mesh: gx: 2 (over x), gy: 4 (over z), gz: 4 (over y, core).
Axes of the slice: x: 2, y: 2, z: 4, core: 2. Of those that a mesh axis runs over, the one named last changes fastest.
Arguments:
- acts: bfloat16 [40960, 768], P(('gx', 'gy', 'gz')), may hold values from -6 to 6
- grads_out: bfloat16 [40960, 768], P(('gx', 'gy', 'gz')), may hold values from -0.03125 to 0.03125
- master: float32 [4608, 128], P(('gx', 'gy', 'gz')), may hold values from -0.3 to 0.3
- moment: float32 [4608, 128], P(('gx', 'gy', 'gz')), may hold values from -6 to 6
- second: float32 [4608, 128], P(('gx', 'gy', 'gz')), may hold values from 0.1 to 2
Outputs:
- master_new: float32 [4608, 128], P(('gx', 'gy', 'gz'))
- moment_new: float32 [4608, 128], P(('gx', 'gy', 'gz'))
- second_new: float32 [4608, 128], P(('gx', 'gy', 'gz'))
- weights: bfloat16 [768, 768], replicated
All inputs are finite; a program needn't handle non-finite values.
Results may differ from a plain program's by a relative error of at most 0.003.
Values may be sent and summed in bfloat16 or wider, within the bound.
No kernel may reach another device: no remote copies, remote signals or barrier semaphores. Data moves between devices by JAX's collectives and lax.ppermute only.
A program may use at most 64 MiB of HBM per device.

v0:
```python
import jax
import jax.numpy as jnp
from jax import lax
from jax.sharding import PartitionSpec as P

STEP = 1000


def shards(acts, grads_out, master, moment, second):
    width_in = acts.shape[1]
    width_out = grads_out.shape[1]
    lane = master.shape[1]
    total_rows = width_in * width_out // lane
    local_grad = lax.dot_general(
        acts, grads_out, (((0,), (0,)), ((), ())), preferred_element_type=jnp.float32
    )
    local_flat = local_grad.reshape(total_rows, lane)
    partial_value = lax.psum_scatter(
        local_flat.astype(jnp.bfloat16), "gx", scatter_dimension=0, tiled=True
    ).astype(jnp.float32)
    partial_value = lax.psum_scatter(
        partial_value.astype(jnp.bfloat16), "gy", scatter_dimension=0, tiled=True
    ).astype(jnp.float32)
    gradient = lax.psum_scatter(
        partial_value.astype(jnp.bfloat16), "gz", scatter_dimension=0, tiled=True
    ).astype(jnp.float32)
    moment_new = 0.9 * moment + 0.1 * gradient
    second_new = 0.95 * second + 0.05 * gradient * gradient
    first_fix = 1.0 - 0.9**STEP
    second_fix = 1.0 - 0.95**STEP
    ratio = moment_new / first_fix / (jnp.sqrt(second_new / second_fix) + 1e-08)
    master_new = master - 0.01 * (ratio + 0.01 * master)
    rounded = master_new.astype(jnp.bfloat16)
    gathered = lax.all_gather(rounded, "gz", axis=0, tiled=True)
    gathered = lax.all_gather(gathered, "gy", axis=0, tiled=True)
    gathered = lax.all_gather(gathered, "gx", axis=0, tiled=True)
    weights = gathered.reshape(width_in, width_out)
    return (master_new, moment_new, second_new, weights)


def solution(mesh):
    return jax.shard_map(
        shards,
        mesh=mesh,
        in_specs=(
            P(("gx", "gy", "gz"), None),
            P(("gx", "gy", "gz"), None),
            P(("gx", "gy", "gz"), None),
            P(("gx", "gy", "gz"), None),
            P(("gx", "gy", "gz"), None),
        ),
        out_specs=(
            P(("gx", "gy", "gz"), None),
            P(("gx", "gy", "gz"), None),
            P(("gx", "gy", "gz"), None),
            P(),
        ),
        check_vma=False,
    )
```

profile of v0, /device:TPU:0, one launch (start us, length us, event | category | flops | bytes accessed | tf_op | source)
XLA Modules:
  0.0 141.0 jit_solution(13236243267090482629)
XLA Ops:
  7.2 0.0 copy-start
  7.2 0.0 reduce-scatter.4.cloned.1.call-start
  7.2 1.5 %copy-done = bf16[1280,768]{1,0:T(8,128)(2,1)S(1)} copy-done((bf16[1280,768]{1,0:T(8,128)(2,1)S(1)}, bf16[1280,768]{1,0:T(8,128)(2,1)}, u32[]{:S(2)}) %copy-start) | copy-done | bytes 1966104
  8.7 3.3 %convolution_convert_fusion = bf16[768,768]{1,0:T(8,128)(2,1)S(1)} fusion(bf16[1280,768]{1,0:T(8,128)(2,1)S(1)} %copy-done, bf16[1280,768]{1,0:T(8,128)(2,1)} %param.6), kind=kOutput, calls=%fused_computation | convolution fusion | flops 1510539264 | bytes 5111808 | tf_op jit(solution)/shard_map/dot_general | solution.py:14
  12.0 0.0 copy-start.1
  12.0 0.0 copy-start.2
  12.0 0.0 copy-start.3
  12.1 1.9 %convert_element_type.17 = bf16[4608,128]{1,0:T(8,128)(2,1)} reshape(bf16[768,768]{1,0:T(8,128)(2,1)S(1)} %convolution_convert_fusion) | data formatting | bytes 2359296 | tf_op jit(solution)/shard_map/convert_element_type | solution.py:19
  13.9 0.0 reduce-scatter.4.cloned.1.call-update
  13.9 0.0 reduce-scatter.6.cloned.1.call-start
  14.0 24.7 %reduce-scatter.4.cloned.1.call-done = bf16[2304,128]{1,0:T(8,128)(2,1)} async-done(((bf16[4608,128]{1,0:T(8,128)(2,1)}), bf16[2304,128]{1,0:T(8,128)(2,1)}) %reduce-scatter.4.cloned.1.call-update) | async-done | bytes 589840 | tf_op jit(solution)/shard_map/reduce_scatter | solution.py:18
  38.7 0.0 reduce-scatter.6.cloned.1.call-update
  38.7 0.0 reduce-scatter.8.cloned.1.call-start
  38.7 24.4 %reduce-scatter.6.cloned.1.call-done = bf16[576,128]{1,0:T(8,128)(2,1)} async-done(((bf16[2304,128]{1,0:T(8,128)(2,1)}), bf16[576,128]{1,0:T(8,128)(2,1)}) %reduce-scatter.6.cloned.1.call-update) | async-done | bytes 147472 | tf_op jit(solution)/shard_map/reduce_scatter | solution.py:21
  63.1 0.0 reduce-scatter.8.cloned.1.call-update
  63.1 0.0 all-gather.2.cloned.1.call-start
  63.2 20.5 %reduce-scatter.8.cloned.1.call-done = bf16[144,128]{1,0:T(8,128)(2,1)} async-done(((bf16[576,128]{1,0:T(8,128)(2,1)}), bf16[144,128]{1,0:T(8,128)(2,1)}) %reduce-scatter.8.cloned.1.call-update) | async-done | bytes 36880 | tf_op jit(solution)/shard_map/reduce_scatter | solution.py:24
  83.7 0.0 copy-done.1
  83.7 0.0 copy-done.2
  83.7 0.0 copy-done.3
  83.7 1.5 %fusion.2 = (bf16[144,128]{1,0:T(8,128)(2,1)S(1)}, f32[144,128]{1,0:T(8,128)}, f32[144,128]{1,0:T(8,128)}, f32[144,128]{1,0:T(8,128)}) fusion(f32[144,128]{1,0:T(8,128)S(1)} %copy-done.1, bf16[144,128]{1,0:T(8,128)(2,1)} %reduce-scatter.8.cloned.1.call-done, f32[144,128]{1,0:T(8,128)S(1)} %copy-done.2, f32[144,128]{1,0:T(8,128)S(1)} %copy-done.3), kind=kLoop, calls=%fused_computation.6 | loop fusion | flops 276480 | bytes 516096 | tf_op jit(solution)/shard_map/convert_element_type | solution.py:33
  85.2 5.4 %all_gather.9 = bf16[576,128]{1,0:T(8,128)(2,1)S(1)} all-gather(bf16[144,128]{1,0:T(8,128)(2,1)S(1)} %get-tuple-element.4), channel_id=1, replica_groups=mesh['gx'=2,'gy'=4,'gz'=4] {'gz'}, dimensions={0}, use_global_device_ids=true | all-gather | bytes 184320 | tf_op jit(solution)/shard_map/all_gather | solution.py:34
  90.6 17.2 %all_gather.10 = bf16[2304,128]{1,0:T(8,128)(2,1)} all-gather(bf16[576,128]{1,0:T(8,128)(2,1)S(1)} %all_gather.9), channel_id=1, replica_groups=mesh['gx'=2,'gy'=4,'gz'=4] {'gy'}, dimensions={0}, use_global_device_ids=true | all-gather | bytes 737280 | tf_op jit(solution)/shard_map/all_gather | solution.py:35
  107.8 0.0 all-gather.2.cloned.1.call-update
  107.8 23.3 %all-gather.2.cloned.1.call-done = bf16[4608,128]{1,0:T(8,128)(2,1)} async-done(((bf16[2304,128]{1,0:T(8,128)(2,1)}), bf16[4608,128]{1,0:T(8,128)(2,1)}) %all-gather.2.cloned.1.call-update) | async-done | bytes 1179664 | tf_op jit(solution)/shard_map/all_gather | solution.py:36
  131.1 3.3 %reshape.13 = bf16[768,768]{1,0:T(8,128)(2,1)} reshape(bf16[4608,128]{1,0:T(8,128)(2,1)} %all-gather.2.cloned.1.call-done) | data formatting | bytes 2359296 | tf_op jit(solution)/shard_map/reshape | solution.py:37
Async XLA Ops:
  7.2 1.6 %copy-start = (bf16[1280,768]{1,0:T(8,128)(2,1)S(1)}, bf16[1280,768]{1,0:T(8,128)(2,1)}, u32[]{:S(2)}) copy-start(bf16[1280,768]{1,0:T(8,128)(2,1)} %param.5) | copy-start | bytes 5898244
  7.2 31.5 %reduce-scatter.4.cloned.1.call-start = ((), (), s32[]{:S(2)}) async-start(), calls=%async_computation.3 | async-start | bytes 1769472 | tf_op jit(solution)/shard_map/reduce_scatter | solution.py:18
  12.0 71.7 %copy-start.1 = (f32[144,128]{1,0:T(8,128)S(1)}, f32[144,128]{1,0:T(8,128)}, u32[]{:S(2)}) copy-start(f32[144,128]{1,0:T(8,128)} %param.7) | copy-start | bytes 221188
  12.0 71.7 %copy-start.2 = (f32[144,128]{1,0:T(8,128)S(1)}, f32[144,128]{1,0:T(8,128)}, u32[]{:S(2)}) copy-start(f32[144,128]{1,0:T(8,128)} %param.9) | copy-start | bytes 221188
  12.0 71.7 %copy-start.3 = (f32[144,128]{1,0:T(8,128)S(1)}, f32[144,128]{1,0:T(8,128)}, u32[]{:S(2)}) copy-start(f32[144,128]{1,0:T(8,128)} %param.8) | copy-start | bytes 221188
  13.9 49.2 %reduce-scatter.6.cloned.1.call-start = ((), (), s32[]{:S(2)}) async-start(), calls=%async_computation.4 | async-start | bytes 737280 | tf_op jit(solution)/shard_map/reduce_scatter | solution.py:21
  38.7 45.0 %reduce-scatter.8.cloned.1.call-start = ((), (), s32[]{:S(2)}) async-start(), calls=%async_computation.5 | async-start | bytes 184320 | tf_op jit(solution)/shard_map/reduce_scatter | solution.py:24
  63.1 68.0 %all-gather.2.cloned.1.call-start = ((), (), s32[]{:S(2)}) async-start(), calls=%async_computation.6 | async-start | bytes 1769472 | tf_op jit(solution)/shard_map/all_gather | solution.py:36
Sparse Core Ops, SparseCore 0:
  14.1 24.5 reduce-scatter.3
  40.9 22.1 reduce-scatter.5
  65.5 18.1 reduce-scatter.7
  108.0 23.0 all-gather.1
where the time goes:
time: 141 us
  waiting for transfers between devices  92.9 us (66%)
  blocking collectives  22.6 us (16%)
  between operations  13.8 us (10%)
  local copies, waits for them, and re-layouts  6.73 us (5%)
  matrix products  3.29 us (2%)
  other arithmetic  1.48 us (1%)
    reduce_scatter x1, waiting for transfers between devices, shards(): lax.psum_scatter(local_flat.astype(jnp.bfloat16), 'gx', scatter_dimension...  24.7 us
    reduce_scatter x1, waiting for transfers between devices, shards(): lax.psum_scatter(partial_value.astype(jnp.bfloat16), 'gy', scatter_dimens...  24.4 us
    all_gather x1, waiting for transfers between devices, shards(): gathered = lax.all_gather(gathered, 'gx', axis=0, tiled=True)  23.3 us
    reduce_scatter x1, waiting for transfers between devices, shards(): lax.psum_scatter(partial_value.astype(jnp.bfloat16), 'gz', scatter_dimens...  20.5 us
    all_gather x1, blocking collectives, shards(): gathered = lax.all_gather(gathered, 'gy', axis=0, tiled=True)  17.2 us
    all_gather x1, blocking collectives, shards(): gathered = lax.all_gather(rounded, 'gz', axis=0, tiled=True)  5.45 us
    reshape x1, local copies, waits for them, and re-layouts, shards(): weights = gathered.reshape(width_in, width_out)  3.35 us
    dot_general x1, matrix products, shards(): lax.dot_general(acts, grads_out, (((0,), (0,)), ((), ())), preferred_elem...  3.29 us
  transfers between devices with their start and end apart: 4, of which 4 were waited for; matrix products, arithmetic and copies ran while one was open for 0% of the time, Pallas kernels for 0%

commit v1 on v0

v1 whole, which is shorter than its diff:
```python
import functools

import jax
import jax.numpy as jnp
from jax import lax
from jax.experimental import pallas as pl
from jax.experimental.pallas import tpu as pltpu
from jax.sharding import Mesh, PartitionSpec as P

STEP = 1000
AXES = ("gx", "gy", "gz")
SPLIT = ("gx", "gy", "gr", "gc")
BF16, F32 = jnp.bfloat16, jnp.float32
VMEM = pl.BlockSpec(memory_space=pltpu.VMEM)
ANY = pl.BlockSpec(memory_space=pl.ANY)


def adam(gradient, master, moment, second):
    moment_new = 0.9 * moment + 0.1 * gradient
    second_new = 0.95 * second + 0.05 * gradient * gradient
    first_fix = 1.0 - 0.9**STEP
    second_fix = 1.0 - 0.95**STEP
    ratio = moment_new / first_fix / (jnp.sqrt(second_new / second_fix) + 1e-08)
    master_new = master - 0.01 * (ratio + 0.01 * master)
    return master_new, moment_new, second_new


def shards(acts, grads_out, master, moment, second):
    width_in = acts.shape[1]
    width_out = grads_out.shape[1]
    lane = master.shape[1]
    total_rows = width_in * width_out // lane
    local_grad = lax.dot_general(
        acts, grads_out, (((0,), (0,)), ((), ())), preferred_element_type=F32
    )
    value = local_grad.reshape(total_rows, lane)
    for axis in AXES:
        value = lax.psum_scatter(
            value.astype(BF16), axis, scatter_dimension=0, tiled=True
        ).astype(F32)
    master_new, moment_new, second_new = adam(value, master, moment, second)
    gathered = master_new.astype(BF16)
    for axis in AXES[::-1]:
        gathered = lax.all_gather(gathered, axis, axis=0, tiled=True)
    return (master_new, moment_new, second_new, gathered.reshape(width_in, width_out))


def here():
    return tuple(lax.axis_index(axis) for axis in SPLIT)


def struct(shape, dtype):
    return jax.ShapeDtypeStruct(shape, dtype)


def matmul_kernel(sizes, rows, a, g, send, keep):
    nx, nz, nr = sizes
    mx, mz, mr, mc = here()
    product = lax.dot_general(
        a[...], g[...], (((0,), (0,)), ((), ())), preferred_element_type=F32
    ).astype(BF16)

    def place(own):
        for block in range(nx * nz * nr * 2):
            c, r = block % 2, block // 2 % nr
            z, x = block // (2 * nr) % nz, block // (2 * nr * nz)
            target = keep if c == own else send
            target[(x ^ mx) * nr + (r ^ mr), z ^ mz] = product[
                rows * block : rows * (block + 1)
            ]

    for own in range(2):
        pl.when(mc == own)(functools.partial(place, own))


def split_kernel(n_in, kept, *refs):
    arrivals, pieces = refs[:n_in], refs[n_in:]
    for k, piece in enumerate(pieces):
        total = kept[k].astype(F32)
        for arrival in arrivals:
            total += arrival[k].astype(F32)
        piece[...] = total.astype(piece.dtype)


def split(name, kept, arrivals):
    n, shape = kept.shape[0], kept.shape[1:]
    return pl.pallas_call(
        functools.partial(split_kernel, len(arrivals)),
        in_specs=[VMEM] * (1 + len(arrivals)),
        out_specs=[VMEM] * n,
        out_shape=[struct(shape, F32)] + [struct(shape, BF16)] * (n - 1),
        name=name,
    )(kept, *arrivals)


def adam_kernel(n_in, rows, per_row, lane, kept, *refs):
    arrivals = refs[:n_in]
    master, moment, second = refs[n_in : n_in + 3]
    master_new, moment_new, second_new, weights, flat = refs[n_in + 3 :]
    total = kept[...].astype(F32)
    for arrival in arrivals:
        total += arrival[...].astype(F32)
    for j in range(per_row):
        flat[pl.ds(j, rows, stride=per_row), :] = total[:, j * lane : (j + 1) * lane]
    values = adam(flat[...], master[...], moment[...], second[...])
    master_new[...], moment_new[...], second_new[...] = values
    flat[...] = values[0]
    for j in range(per_row):
        weights[:, j * lane : (j + 1) * lane] = flat[
            pl.ds(j, rows, stride=per_row), :
        ].astype(BF16)


def stack_kernel(axis, *refs):
    pieces, out = refs[:-1], refs[-1]
    me = lax.axis_index(axis)
    for k, piece in enumerate(pieces):
        out[me ^ k] = piece[...]


def place_kernel(sizes, rows, own, other, out, sem):
    nx, nz, nr = sizes
    mc = lax.axis_index("gc")

    def copies(first):
        for block in range(nx * nz * nr * 2):
            c, r = block % 2, block // 2 % nr
            z, x = block // (2 * nr) % nz, block // (2 * nr * nz)
            source = own if c == first else other
            yield pltpu.make_async_copy(
                source.at[x * nr + r, z], out.at[pl.ds(rows * block, rows)], sem
            )

    def run(first):
        for copy in copies(first):
            copy.start()
        for copy in copies(first):
            copy.wait()

    for first in range(2):
        pl.when(mc == first)(functools.partial(run, first))


def fast(sizes, acts, grads_out, master, moment, second):
    nx, nz, nr = sizes
    width_in, width_out = acts.shape[1], grads_out.shape[1]
    own_rows, lane = master.shape
    per_row = width_out // lane
    rows = own_rows // per_row
    group = nx * nr

    def permute(value, dx=0, dz=0, dr=0, dc=0):
        pairs = []
        for x in range(nx):
            for z in range(nz):
                for r in range(nr):
                    for c in range(2):
                        source = ((x * nz + z) * nr + r) * 2 + c
                        target = (((x ^ dx) * nz + (z ^ dz)) * nr + (r ^ dr)) * 2
                        pairs.append((source, target + (c ^ dc)))
        return lax.ppermute(value, SPLIT, pairs)

    half = struct((group, nz, rows, width_out), BF16)
    send, keep = pl.pallas_call(
        functools.partial(matmul_kernel, sizes, rows),
        in_specs=[VMEM] * 2,
        out_specs=[VMEM] * 2,
        out_shape=[half] * 2,
        name="matmul",
    )(acts, grads_out)
    kept, *pieces = split("split_core", keep, [permute(send, dc=1)])
    arrivals = [
        permute(piece, dx=k // nr, dr=k % nr) for k, piece in enumerate(pieces, 1)
    ]
    kept, *pieces = split("split_plane", kept, arrivals)
    arrivals = [permute(piece, dz=k) for k, piece in enumerate(pieces, 1)]
    state = struct((own_rows, lane), F32)
    master_new, moment_new, second_new, weights = pl.pallas_call(
        functools.partial(adam_kernel, len(arrivals), rows, per_row, lane),
        in_specs=[VMEM] * (4 + len(arrivals)),
        out_specs=[VMEM] * 4,
        out_shape=[state] * 3 + [struct((rows, width_out), BF16)],
        scratch_shapes=[pltpu.VMEM((own_rows, lane), F32)],
        name="adam",
    )(kept, *arrivals, master, moment, second)
    line = pl.pallas_call(
        functools.partial(stack_kernel, "gy"),
        in_specs=[VMEM] * nz,
        out_specs=VMEM,
        out_shape=struct((nz, rows, width_out), BF16),
        name="stack_line",
    )(weights, *[permute(weights, dz=k) for k in range(1, nz)])
    own = lax.all_gather(line, ("gx", "gr"), axis=0)
    out = pl.pallas_call(
        functools.partial(place_kernel, sizes, rows),
        in_specs=[ANY] * 2,
        out_specs=ANY,
        out_shape=struct((width_in, width_out), BF16),
        scratch_shapes=[pltpu.SemaphoreType.DMA],
        name="place",
    )(own, permute(own, dc=1))
    return master_new, moment_new, second_new, out


def power_of_two(n):
    return n & (n - 1) == 0


def chosen(mesh, sizes, *args):
    acts, grads_out, master = args[:3]
    width_in, width_out = acts.shape[1], grads_out.shape[1]
    even = all(power_of_two(n) for n in sizes) and mesh.shape["gz"] % 2 == 0
    whole = width_in % (8 * mesh.size) == 0 and width_out % master.shape[1] == 0
    if not (even and whole):
        spec = P(AXES, None)
        return jax.shard_map(
            shards, mesh=mesh, in_specs=(spec,) * 5,
            out_specs=(spec,) * 3 + (P(),), check_vma=False,
        )(*args)
    spec = P(SPLIT, None)
    finer = Mesh(mesh.devices.reshape(*sizes, 2), SPLIT)
    return jax.shard_map(
        functools.partial(fast, sizes), mesh=finer, in_specs=(spec,) * 5,
        out_specs=(spec,) * 3 + (P(),), check_vma=False,
    )(*args)


def solution(mesh):
    sizes = (mesh.shape["gx"], mesh.shape["gy"], mesh.shape["gz"] // 2)
    return functools.partial(chosen, mesh, sizes)
```

time: 141 us -> 97.2 us (0.69)
  waiting for transfers between devices: 92.9 us -> 19.2 us
  Pallas kernels: 0 us -> 49.2 us
  starting transfers between devices: 0.16 us -> 13.7 us
  between operations: 13.8 us -> 0.67 us
  blocking collectives: 22.6 us -> 10.6 us
  matrix products: 3.29 us -> 0 us
  local copies, waits for them, and re-layouts: 6.73 us -> 3.54 us
  other arithmetic: 1.48 us -> 0 us
    reduce_scatter x3 -> x0, waiting for transfers between devices: 69.6 us -> none  [the longest x1 24.7 us: shards(): lax.psum_scatter(local_flat.astype(jnp.bfloat16), 'gx', scatter_dimension...]
    pallas_call x0 -> x6, Pallas kernels: none -> 49.2 us  [the longest x1 36.8 us: fast(): pl.pallas_call(functools.partial(place_kernel, sizes, rows), in_specs=[AN...]
    all_gather x1 -> x0, waiting for transfers between devices: 23.3 us -> none  [shards(): gathered = lax.all_gather(gathered, 'gx', axis=0, tiled=True)]
    ppermute x0 -> x11, waiting for transfers between devices: none -> 19.2 us  [permute(): return lax.ppermute(value, SPLIT, pairs)]
    ppermute x0 -> x11, starting transfers between devices: none -> 13.7 us  [permute(): return lax.ppermute(value, SPLIT, pairs)]
    all_gather x2 -> x1, blocking collectives: 22.6 us -> 10.6 us  [fast(): own = lax.all_gather(line, ('gx', 'gr'), axis=0)]
    reshape x1 -> x0, local copies, waits for them, and re-layouts: 3.35 us -> none  [shards(): weights = gathered.reshape(width_in, width_out)]
    dot_general x1 -> x0, matrix products: 3.29 us -> none  [shards(): lax.dot_general(acts, grads_out, (((0,), (0,)), ((), ())), preferred_elem...]
  transfers between devices with their start and end apart: 4 -> 11, of which waited for: 4 -> 9; matrix products, arithmetic and copies ran while one was open for 0% -> 0% of each run, Pallas kernels for 0% -> 0%
where the time goes in v1:
time: 97.2 us; the launch traced here: 96.9 us
  Pallas kernels  49.2 us (51%)
  waiting for transfers between devices  19.2 us (20%)
  starting transfers between devices  13.7 us (14%)
  blocking collectives  10.6 us (11%)
  local copies, waits for them, and re-layouts  3.54 us (4%)
    pallas_call x1, Pallas kernels, fast(): pl.pallas_call(functools.partial(place_kernel, sizes, rows), in_specs=[AN...  36.8 us
    ppermute x11, waiting for transfers between devices, permute(): return lax.ppermute(value, SPLIT, pairs)  19.2 us
    ppermute x11, starting transfers between devices, permute(): return lax.ppermute(value, SPLIT, pairs)  13.7 us
    all_gather x1, blocking collectives, fast(): own = lax.all_gather(line, ('gx', 'gr'), axis=0)  10.6 us
    pallas_call x1, Pallas kernels, fast(): pl.pallas_call(functools.partial(matmul_kernel, sizes, rows), in_specs=[V...  5.04 us
    pallas_call x2, Pallas kernels, split(): pl.pallas_call(functools.partial(split_kernel, len(arrivals)), in_specs=[...  4 us
    unnamed x24, local copies, waits for them, and re-layouts  3.54 us
  transfers between devices with their start and end apart: 11, of which 9 were waited for; matrix products, arithmetic and copies ran while one was open for 0% of the time, Pallas kernels for 0%

profile of v1, /device:TPU:0, one launch (start us, length us, event | category | flops | bytes accessed | tf_op | source)
XLA Modules:
  0.0 96.9 jit_solution(4053223812429342877)
XLA Ops:
  0.6 5.0 %matmul.1 = (bf16[4,4,24,768]{3,2,1,0:T(8,128)(2,1)}, bf16[4,4,24,768]{3,2,1,0:T(8,128)(2,1)}) custom-call(bf16[1280,768]{1,0:T(8,128)(2,1)} %a.1, bf16[1280,768]{1,0:T(8,128)(2,1)} %g.1), custom_call_target="tpu_custom_call" | custom-call | tf_op jit(solution)/shard_map/matmul/pallas_call | solution.py:164
  5.7 0.5 collective-permute-start
  6.2 1.8 %collective-permute-done.refs_0_ = bf16[4,4,24,768]{3,2,1,0:T(8,128)(2,1)S(1)} collective-permute-done((bf16[4,4,24,768]{3,2,1,0:T(8,128)(2,1)}, bf16[4,4,24,768]{3,2,1,0:T(8,128)(2,1)S(1)}, u32[]{:S(2)}, u32[]{:S(2)}) %collective-permute-start) | collective-permute-done | bytes 589856 | tf_op jit(solution)/shard_map/ppermute | solution.py:161
  8.0 0.8 copy-done.1
  8.8 2.2 %split_core.1 = (f32[4,24,768]{2,1,0:T(8,128)}, bf16[4,24,768]{2,1,0:T(8,128)(2,1)}, bf16[4,24,768]{2,1,0:T(8,128)(2,1)}, bf16[4,24,768]{2,1,0:T(8,128)(2,1)}) custom-call(bf16[4,4,24,768]{3,2,1,0:T(8,128)(2,1)} %get-tuple-element.18.kept, bf16[4,4,24,768]{3,2,1,0:T(8,128)(2,1)} %copy-done.1), custom_call_target="tpu_custom_call" | custom-call | tf_op jit(solution)/shard_map/split_core/pallas_call | solution.py:87
  11.0 2.9 %collective-permute-start.1 = (bf16[4,24,768]{2,1,0:T(8,128)(2,1)}, bf16[4,24,768]{2,1,0:T(8,128)(2,1)S(1)}, u32[]{:S(2)}, u32[]{:S(2)}) collective-permute-start(bf16[4,24,768]{2,1,0:T(8,128)(2,1)} %get-tuple-element.21), channel_id=1, source_target_pairs={{0,2},{1,3},{2,0},{3,1},{4,6},{5,7},{6,4},{7,5},{8,10},{9,11},{10,... | collective-permute-start | bytes 442376 | tf_op jit(solution)/shard_map/ppermute | solution.py:161
  13.9 1.5 %collective-permute-start.2 = (bf16[4,24,768]{2,1,0:T(8,128)(2,1)}, bf16[4,24,768]{2,1,0:T(8,128)(2,1)S(1)}, u32[]{:S(2)}, u32[]{:S(2)}) collective-permute-start(bf16[4,24,768]{2,1,0:T(8,128)(2,1)} %get-tuple-element.22), channel_id=1, source_target_pairs={{0,16},{1,17},{2,18},{3,19},{4,20},{5,21},{6,22},{7,23},{8,24},{9,... | collective-permute-start | bytes 442376 | tf_op jit(solution)/shard_map/ppermute | solution.py:161
  15.4 2.9 %collective-permute-done.1.refs_0_ = bf16[4,24,768]{2,1,0:T(8,128)(2,1)S(1)} collective-permute-done((bf16[4,24,768]{2,1,0:T(8,128)(2,1)}, bf16[4,24,768]{2,1,0:T(8,128)(2,1)S(1)}, u32[]{:S(2)}, u32[]{:S(2)}) %collective-permute-start.1) | collective-permute-done | bytes 147488 | tf_op jit(solution)/shard_map/ppermute | solution.py:161
  18.2 2.6 %collective-permute-done.2.refs_1_ = bf16[4,24,768]{2,1,0:T(8,128)(2,1)S(1)} collective-permute-done((bf16[4,24,768]{2,1,0:T(8,128)(2,1)}, bf16[4,24,768]{2,1,0:T(8,128)(2,1)S(1)}, u32[]{:S(2)}, u32[]{:S(2)}) %collective-permute-start.2) | collective-permute-done | bytes 147488 | tf_op jit(solution)/shard_map/ppermute | solution.py:161
  20.8 1.8 %collective-permute-done.3.refs_2_ = bf16[4,24,768]{2,1,0:T(8,128)(2,1)S(1)} collective-permute-done((bf16[4,24,768]{2,1,0:T(8,128)(2,1)}, bf16[4,24,768]{2,1,0:T(8,128)(2,1)S(1)}, u32[]{:S(2)}, u32[]{:S(2)}) %collective-permute-start.3) | collective-permute-done | bytes 147488 | tf_op jit(solution)/shard_map/ppermute | solution.py:161
  22.6 0.6 copy-done.5
  23.2 1.8 %split_plane.1 = (f32[24,768]{1,0:T(8,128)}, bf16[24,768]{1,0:T(8,128)(2,1)}, bf16[24,768]{1,0:T(8,128)(2,1)}, bf16[24,768]{1,0:T(8,128)(2,1)}) custom-call(f32[4,24,768]{2,1,0:T(8,128)} %get-tuple-element.20.kept, bf16[4,24,768]{2,1,0:T(8,128)(2,1)} %copy-done.3, bf16[4,24,768]{2,1,0:T(8,128)(2,1)} %copy-done.4, bf16[4,24,768]{2,1,0:T(8,128)(2,1)} %copy-done.5), custom_call_target="tpu_custom_call" | custom-call | tf_op jit(solution)/shard_map/split_plane/pallas_call | solution.py:87
  25.0 1.8 %collective-permute-start.4 = (bf16[24,768]{1,0:T(8,128)(2,1)}, bf16[24,768]{1,0:T(8,128)(2,1)S(1)}, u32[]{:S(2)}, u32[]{:S(2)}) collective-permute-start(bf16[24,768]{1,0:T(8,128)(2,1)} %get-tuple-element.25), channel_id=1, source_target_pairs={{0,4},{1,5},{2,6},{3,7},{4,0},{5,1},{6,2},{7,3},{8,12},{9,13},{10,... | collective-permute-start | bytes 110600 | tf_op jit(solution)/shard_map/ppermute | solution.py:161
  26.8 2.6 %collective-permute-start.5 = (bf16[24,768]{1,0:T(8,128)(2,1)}, bf16[24,768]{1,0:T(8,128)(2,1)S(1)}, u32[]{:S(2)}, u32[]{:S(2)}) collective-permute-start(bf16[24,768]{1,0:T(8,128)(2,1)} %get-tuple-element.26), channel_id=1, source_target_pairs={{0,8},{1,9},{2,10},{3,11},{4,12},{5,13},{6,14},{7,15},{8,0},{9,1},... | collective-permute-start | bytes 110600 | tf_op jit(solution)/shard_map/ppermute | solution.py:161
  29.4 0.0 collective-permute-start.6
  29.4 0.0 collective-permute-done.4.refs_0_
  29.4 2.8 %collective-permute-done.5.refs_1_ = bf16[24,768]{1,0:T(8,128)(2,1)S(1)} collective-permute-done((bf16[24,768]{1,0:T(8,128)(2,1)}, bf16[24,768]{1,0:T(8,128)(2,1)S(1)}, u32[]{:S(2)}, u32[]{:S(2)}) %collective-permute-start.5) | collective-permute-done | bytes 36896 | tf_op jit(solution)/shard_map/ppermute | solution.py:161
  32.3 3.1 %collective-permute-done.6.refs_2_ = bf16[24,768]{1,0:T(8,128)(2,1)S(1)} collective-permute-done((bf16[24,768]{1,0:T(8,128)(2,1)}, bf16[24,768]{1,0:T(8,128)(2,1)S(1)}, u32[]{:S(2)}, u32[]{:S(2)}) %collective-permute-start.6) | collective-permute-done | bytes 36896 | tf_op jit(solution)/shard_map/ppermute | solution.py:161
  35.4 0.6 copy-done.8
  36.0 1.8 %adam.1 = (f32[144,128]{1,0:T(8,128)}, f32[144,128]{1,0:T(8,128)}, f32[144,128]{1,0:T(8,128)}, bf16[24,768]{1,0:T(8,128)(2,1)}) custom-call(f32[24,768]{1,0:T(8,128)} %get-tuple-element.24.kept, bf16[24,768]{1,0:T(8,128)(2,1)} %copy-done.6, bf16[24,768]{1,0:T(8,128)(2,1)} %copy-done.7, bf16[24,768]{1,0:T(8,128)(2,1)} %copy-done.8, f32[144,128]{1,0:T(8,128)} %refs_3_.1, ...), custom_call_target="tpu_custom_call" | custom-call | tf_op jit(solution)/shard_map/adam/pallas_call | solution.py:178
  37.8 0.4 collective-permute-start.9
  38.2 4.0 %collective-permute-start.7 = (bf16[24,768]{1,0:T(8,128)(2,1)}, bf16[24,768]{1,0:T(8,128)(2,1)S(1)}, u32[]{:S(2)}, u32[]{:S(2)}) collective-permute-start(bf16[24,768]{1,0:T(8,128)(2,1)} %get-tuple-element.31.refs_0_), channel_id=1, source_target_pairs={{0,4},{1,5},{2,6},{3,7},{4,0},{5,1},{6,2},{7,3},{8,12},{9,13},{10,... | collective-permute-start | bytes 110600 | tf_op jit(solution)/shard_map/ppermute | solution.py:161
  42.2 1.6 %collective-permute-done.9.refs_3_ = bf16[24,768]{1,0:T(8,128)(2,1)S(1)} collective-permute-done((bf16[24,768]{1,0:T(8,128)(2,1)}, bf16[24,768]{1,0:T(8,128)(2,1)S(1)}, u32[]{:S(2)}, u32[]{:S(2)}) %collective-permute-start.9) | collective-permute-done | bytes 36896 | tf_op jit(solution)/shard_map/ppermute | solution.py:161
  43.8 0.6 collective-permute-done.7.refs_1_
  44.4 0.0 copy-done.10
  44.4 0.6 copy-done.11
  45.0 1.5 %stack_line.1 = bf16[4,24,768]{2,1,0:T(8,128)(2,1)} custom-call(bf16[24,768]{1,0:T(8,128)(2,1)} %get-tuple-element.31.refs_0_, bf16[24,768]{1,0:T(8,128)(2,1)} %copy-done.11, bf16[24,768]{1,0:T(8,128)(2,1)} %copy-done.10, bf16[24,768]{1,0:T(8,128)(2,1)} %copy-done.9), custom_call_target="tpu_custom_call" | custom-call | tf_op jit(solution)/shard_map/stack_line/pallas_call | solution.py:186
  46.5 10.6 %all-gather = bf16[16,24,768]{2,1,0:T(8,128)(2,1)S(1)} all-gather(bf16[4,24,768]{2,1,0:T(8,128)(2,1)} %stack_line.1), channel_id=2, replica_groups=mesh['gx'=2,'gy'=4,'gr'=2,'gc'=2] {'gx','gr'}, dimensions={0}, use_global_device_ids=true | all-gather | bytes 737280 | tf_op jit(solution)/shard_map/all_gather | solution.py:193
  57.1 0.1 collective-permute-start.10
  57.2 2.0 %collective-permute-done.10.other = bf16[4,4,24,768]{3,2,1,0:T(8,128)(2,1)S(1)} collective-permute-done((bf16[4,4,24,768]{3,2,1,0:T(8,128)(2,1)S(1)}, bf16[4,4,24,768]{3,2,1,0:T(8,128)(2,1)S(1)}, u32[]{:S(2)}, u32[]{:S(2)}) %collective-permute-start.10) | collective-permute-done | bytes 589856 | tf_op jit(solution)/shard_map/ppermute | solution.py:161
  59.2 0.8 copy-done.2
  60.0 36.8 %place.1 = bf16[768,768]{1,0:T(8,128)(2,1)} custom-call(bf16[4,4,24,768]{3,2,1,0:T(8,128)(2,1)} %bitcast.2, bf16[4,4,24,768]{3,2,1,0:T(8,128)(2,1)} %copy-done.2), custom_call_target="tpu_custom_call" | custom-call | tf_op jit(solution)/shard_map/place/pallas_call | solution.py:194
  (21 shorter events, 0.0 us)
Async XLA Ops:
  5.7 2.3 %collective-permute-start = (bf16[4,4,24,768]{3,2,1,0:T(8,128)(2,1)}, bf16[4,4,24,768]{3,2,1,0:T(8,128)(2,1)S(1)}, u32[]{:S(2)}, u32[]{:S(2)}) collective-permute-start(bf16[4,4,24,768]{3,2,1,0:T(8,128)(2,1)} %get-tuple-element.19), channel_id=1, source_target_pairs={{0,1},{1,0},{2,3},{3,2},{4,5},{5,4},{6,7},{7,6},{8,9},{9,8},{10,11... | collective-permute-start | bytes 1769480 | tf_op jit(solution)/shard_map/ppermute | solution.py:161
  8.0 0.8 copy-start.1
  11.0 7.2 %collective-permute-start.1 = (bf16[4,24,768]{2,1,0:T(8,128)(2,1)}, bf16[4,24,768]{2,1,0:T(8,128)(2,1)S(1)}, u32[]{:S(2)}, u32[]{:S(2)}) collective-permute-start(bf16[4,24,768]{2,1,0:T(8,128)(2,1)} %get-tuple-element.21), channel_id=1, source_target_pairs={{0,2},{1,3},{2,0},{3,1},{4,6},{5,7},{6,4},{7,5},{8,10},{9,11},{10,... | collective-permute-start | bytes 442376 | tf_op jit(solution)/shard_map/ppermute | solution.py:161
  13.9 6.9 %collective-permute-start.2 = (bf16[4,24,768]{2,1,0:T(8,128)(2,1)}, bf16[4,24,768]{2,1,0:T(8,128)(2,1)S(1)}, u32[]{:S(2)}, u32[]{:S(2)}) collective-permute-start(bf16[4,24,768]{2,1,0:T(8,128)(2,1)} %get-tuple-element.22), channel_id=1, source_target_pairs={{0,16},{1,17},{2,18},{3,19},{4,20},{5,21},{6,22},{7,23},{8,24},{9,... | collective-permute-start | bytes 442376 | tf_op jit(solution)/shard_map/ppermute | solution.py:161
  15.3 7.2 %collective-permute-start.3 = (bf16[4,24,768]{2,1,0:T(8,128)(2,1)}, bf16[4,24,768]{2,1,0:T(8,128)(2,1)S(1)}, u32[]{:S(2)}, u32[]{:S(2)}) collective-permute-start(bf16[4,24,768]{2,1,0:T(8,128)(2,1)} %get-tuple-element.23), channel_id=1, source_target_pairs={{0,18},{1,19},{2,16},{3,17},{4,22},{5,23},{6,20},{7,21},{8,26},{9,... | collective-permute-start | bytes 442376 | tf_op jit(solution)/shard_map/ppermute | solution.py:161
  18.2 4.3 %copy-start.3 = (bf16[4,24,768]{2,1,0:T(8,128)(2,1)}, bf16[4,24,768]{2,1,0:T(8,128)(2,1)S(1)}, u32[]{:S(2)}) copy-start(bf16[4,24,768]{2,1,0:T(8,128)(2,1)S(1)} %collective-permute-done.1.refs_0_) | copy-start | bytes 442372
  20.8 1.8 %copy-start.4 = (bf16[4,24,768]{2,1,0:T(8,128)(2,1)}, bf16[4,24,768]{2,1,0:T(8,128)(2,1)S(1)}, u32[]{:S(2)}) copy-start(bf16[4,24,768]{2,1,0:T(8,128)(2,1)S(1)} %collective-permute-done.2.refs_1_) | copy-start | bytes 442372
  22.6 0.7 copy-start.5
  25.0 4.4 %collective-permute-start.4 = (bf16[24,768]{1,0:T(8,128)(2,1)}, bf16[24,768]{1,0:T(8,128)(2,1)S(1)}, u32[]{:S(2)}, u32[]{:S(2)}) collective-permute-start(bf16[24,768]{1,0:T(8,128)(2,1)} %get-tuple-element.25), channel_id=1, source_target_pairs={{0,4},{1,5},{2,6},{3,7},{4,0},{5,1},{6,2},{7,3},{8,12},{9,13},{10,... | collective-permute-start | bytes 110600 | tf_op jit(solution)/shard_map/ppermute | solution.py:161
  26.8 5.4 %collective-permute-start.5 = (bf16[24,768]{1,0:T(8,128)(2,1)}, bf16[24,768]{1,0:T(8,128)(2,1)S(1)}, u32[]{:S(2)}, u32[]{:S(2)}) collective-permute-start(bf16[24,768]{1,0:T(8,128)(2,1)} %get-tuple-element.26), channel_id=1, source_target_pairs={{0,8},{1,9},{2,10},{3,11},{4,12},{5,13},{6,14},{7,15},{8,0},{9,1},... | collective-permute-start | bytes 110600 | tf_op jit(solution)/shard_map/ppermute | solution.py:161
  29.4 6.0 %collective-permute-start.6 = (bf16[24,768]{1,0:T(8,128)(2,1)}, bf16[24,768]{1,0:T(8,128)(2,1)S(1)}, u32[]{:S(2)}, u32[]{:S(2)}) collective-permute-start(bf16[24,768]{1,0:T(8,128)(2,1)} %get-tuple-element.27), channel_id=1, source_target_pairs={{0,12},{1,13},{2,14},{3,15},{4,8},{5,9},{6,10},{7,11},{8,4},{9,5},... | collective-permute-start | bytes 110600 | tf_op jit(solution)/shard_map/ppermute | solution.py:161
  29.4 6.0 %copy-start.6 = (bf16[24,768]{1,0:T(8,128)(2,1)}, bf16[24,768]{1,0:T(8,128)(2,1)S(1)}, u32[]{:S(2)}) copy-start(bf16[24,768]{1,0:T(8,128)(2,1)S(1)} %collective-permute-done.4.refs_0_) | copy-start | bytes 110596
  32.3 3.2 %copy-start.7 = (bf16[24,768]{1,0:T(8,128)(2,1)}, bf16[24,768]{1,0:T(8,128)(2,1)S(1)}, u32[]{:S(2)}) copy-start(bf16[24,768]{1,0:T(8,128)(2,1)S(1)} %collective-permute-done.5.refs_1_) | copy-start | bytes 110596
  35.4 0.6 copy-start.8
  37.8 6.0 %collective-permute-start.9 = (bf16[24,768]{1,0:T(8,128)(2,1)}, bf16[24,768]{1,0:T(8,128)(2,1)S(1)}, u32[]{:S(2)}, u32[]{:S(2)}) collective-permute-start(bf16[24,768]{1,0:T(8,128)(2,1)} %get-tuple-element.31.refs_0_), channel_id=1, source_target_pairs={{0,12},{1,13},{2,14},{3,15},{4,8},{5,9},{6,10},{7,11},{8,4},{9,5},... | collective-permute-start | bytes 110600 | tf_op jit(solution)/shard_map/ppermute | solution.py:161
  38.2 5.6 %collective-permute-start.8 = (bf16[24,768]{1,0:T(8,128)(2,1)}, bf16[24,768]{1,0:T(8,128)(2,1)S(1)}, u32[]{:S(2)}, u32[]{:S(2)}) collective-permute-start(bf16[24,768]{1,0:T(8,128)(2,1)} %get-tuple-element.31.refs_0_), channel_id=1, source_target_pairs={{0,8},{1,9},{2,10},{3,11},{4,12},{5,13},{6,14},{7,15},{8,0},{9,1},... | collective-permute-start | bytes 110600 | tf_op jit(solution)/shard_map/ppermute | solution.py:161
  38.2 6.2 %collective-permute-start.7 = (bf16[24,768]{1,0:T(8,128)(2,1)}, bf16[24,768]{1,0:T(8,128)(2,1)S(1)}, u32[]{:S(2)}, u32[]{:S(2)}) collective-permute-start(bf16[24,768]{1,0:T(8,128)(2,1)} %get-tuple-element.31.refs_0_), channel_id=1, source_target_pairs={{0,4},{1,5},{2,6},{3,7},{4,0},{5,1},{6,2},{7,3},{8,12},{9,13},{10,... | collective-permute-start | bytes 110600 | tf_op jit(solution)/shard_map/ppermute | solution.py:161
  43.8 0.6 copy-start.9
  43.8 0.6 copy-start.10
  44.4 0.6 copy-start.11
  57.1 2.1 %copy-start = (bf16[16,24,768]{2,1,0:T(8,128)(2,1)}, bf16[16,24,768]{2,1,0:T(8,128)(2,1)S(1)}, u32[]{:S(2)}) copy-start(bf16[16,24,768]{2,1,0:T(8,128)(2,1)S(1)} %all-gather) | copy-start | bytes 1769476
  57.1 2.1 %collective-permute-start.10 = (bf16[4,4,24,768]{3,2,1,0:T(8,128)(2,1)S(1)}, bf16[4,4,24,768]{3,2,1,0:T(8,128)(2,1)S(1)}, u32[]{:S(2)}, u32[]{:S(2)}) collective-permute-start(bf16[4,4,24,768]{3,2,1,0:T(8,128)(2,1)S(1)} %bitcast.1), channel_id=1, source_target_pairs={{0,1},{1,0},{2,3},{3,2},{4,5},{5,4},{6,7},{7,6},{8,9},{9,8},{10,11... | collective-permute-start | bytes 1769480 | tf_op jit(solution)/shard_map/ppermute | solution.py:161
  59.2 0.8 copy-start.2

commit v2 on v1

--- a/solution.py
+++ b/solution.py
@@ -49,8 +49,12 @@
     return tuple(lax.axis_index(axis) for axis in SPLIT)
 
 
+def near(*arrays):
+    return [pltpu.with_memory_space_constraint(a, pltpu.VMEM) for a in arrays]
+
+
 def struct(shape, dtype):
-    return jax.ShapeDtypeStruct(shape, dtype)
+    return pltpu.VMEM(shape, dtype)
 
 
 def matmul_kernel(sizes, rows, a, g, send, keep):
@@ -90,7 +94,7 @@
         out_specs=[VMEM] * n,
         out_shape=[struct(shape, F32)] + [struct(shape, BF16)] * (n - 1),
         name=name,
-    )(kept, *arrivals)
+    )(*near(kept, *arrivals))
 
 
 def adam_kernel(n_in, rows, per_row, lane, kept, *refs):
@@ -174,7 +178,7 @@
     ]
     kept, *pieces = split("split_plane", kept, arrivals)
     arrivals = [permute(piece, dz=k) for k, piece in enumerate(pieces, 1)]
-    state = struct((own_rows, lane), F32)
+    state = jax.ShapeDtypeStruct((own_rows, lane), F32)
     master_new, moment_new, second_new, weights = pl.pallas_call(
         functools.partial(adam_kernel, len(arrivals), rows, per_row, lane),
         in_specs=[VMEM] * (4 + len(arrivals)),
@@ -182,23 +186,23 @@
         out_shape=[state] * 3 + [struct((rows, width_out), BF16)],
         scratch_shapes=[pltpu.VMEM((own_rows, lane), F32)],
         name="adam",
-    )(kept, *arrivals, master, moment, second)
+    )(*near(kept, *arrivals), master, moment, second)
     line = pl.pallas_call(
         functools.partial(stack_kernel, "gy"),
         in_specs=[VMEM] * nz,
         out_specs=VMEM,
         out_shape=struct((nz, rows, width_out), BF16),
         name="stack_line",
-    )(weights, *[permute(weights, dz=k) for k in range(1, nz)])
+    )(*near(weights, *[permute(weights, dz=k) for k in range(1, nz)]))
     own = lax.all_gather(line, ("gx", "gr"), axis=0)
     out = pl.pallas_call(
         functools.partial(place_kernel, sizes, rows),
-        in_specs=[ANY] * 2,
+        in_specs=[VMEM] * 2,
         out_specs=ANY,
-        out_shape=struct((width_in, width_out), BF16),
+        out_shape=jax.ShapeDtypeStruct((width_in, width_out), BF16),
         scratch_shapes=[pltpu.SemaphoreType.DMA],
         name="place",
-    )(own, permute(own, dc=1))
+    )(*near(own, permute(own, dc=1)))
     return master_new, moment_new, second_new, out
 
 

time: 97.2 us -> 50.2 us (0.52)
  Pallas kernels: 49.2 us -> 6.88 us
  local copies, waits for them, and re-layouts: 3.54 us -> 0 us
    pallas_call x1, Pallas kernels: 36.8 us -> 1 us  [fast(): pl.pallas_call(functools.partial(place_kernel, sizes, rows), in_specs=[VM...]
    pallas_call x2, Pallas kernels: 4 us -> 0.21 us  [split(): pl.pallas_call(functools.partial(split_kernel, len(arrivals)), in_specs=[...]
    unnamed x24 -> x0, local copies, waits for them, and re-layouts: 3.54 us -> none
    pallas_call x1, Pallas kernels: 1.5 us -> 0.02 us  [fast(): pl.pallas_call(functools.partial(stack_kernel, 'gy'), in_specs=[VMEM] * n...]
    pallas_call x1, Pallas kernels: 5.04 us -> 3.99 us  [fast(): pl.pallas_call(functools.partial(matmul_kernel, sizes, rows), in_specs=[V...]
where the time goes in v2:
time: 50.2 us; the launch traced here: 50 us
  waiting for transfers between devices  18.3 us (36%)
  starting transfers between devices  13.9 us (28%)
  blocking collectives  10.3 us (21%)
  Pallas kernels  6.88 us (14%)
  between operations  0.66 us (1%)
    ppermute x11, waiting for transfers between devices, permute(): return lax.ppermute(value, SPLIT, pairs)  18.3 us
    ppermute x11, starting transfers between devices, permute(): return lax.ppermute(value, SPLIT, pairs)  13.9 us
    all_gather x1, blocking collectives, fast(): own = lax.all_gather(line, ('gx', 'gr'), axis=0)  10.3 us
    pallas_call x1, Pallas kernels, fast(): pl.pallas_call(functools.partial(matmul_kernel, sizes, rows), in_specs=[V...  3.99 us
    pallas_call x1, Pallas kernels, fast(): pl.pallas_call(functools.partial(adam_kernel, len(arrivals), rows, per_ro...  1.67 us
  transfers between devices with their start and end apart: 11, of which 9 were waited for; matrix products, arithmetic and copies ran while one was open for 0% of the time, Pallas kernels for 0%

profile of v2, /device:TPU:0, one launch (start us, length us, event | category | flops | bytes accessed | tf_op | source)
XLA Modules:
  0.0 50.0 jit_solution(10245187569746150153)
XLA Ops:
  0.6 4.0 %matmul.1 = (bf16[4,4,24,768]{3,2,1,0:T(8,128)(2,1)S(1)}, bf16[4,4,24,768]{3,2,1,0:T(8,128)(2,1)S(1)}) custom-call(bf16[1280,768]{1,0:T(8,128)(2,1)} %a.1, bf16[1280,768]{1,0:T(8,128)(2,1)} %g.1), custom_call_target="tpu_custom_call" | custom-call | tf_op jit(solution)/shard_map/matmul/pallas_call | solution.py:168
  4.6 0.6 %collective-permute-start = (bf16[4,4,24,768]{3,2,1,0:T(8,128)(2,1)S(1)}, bf16[4,4,24,768]{3,2,1,0:T(8,128)(2,1)S(1)}, u32[]{:S(2)}, u32[]{:S(2)}) collective-permute-start(bf16[4,4,24,768]{3,2,1,0:T(8,128)(2,1)S(1)} %get-tuple-element.19), channel_id=1, source_target_pairs={{0,1},{1,0},{2,3},{3,2},{4,5},{5,4},{6,7},{7,6},{8,9},{9,8},{10,11... | collective-permute-start | bytes 1769480 | tf_op jit(solution)/shard_map/ppermute | solution.py:165
  5.2 1.6 %collective-permute-done.refs_0_ = bf16[4,4,24,768]{3,2,1,0:T(8,128)(2,1)S(1)} collective-permute-done((bf16[4,4,24,768]{3,2,1,0:T(8,128)(2,1)S(1)}, bf16[4,4,24,768]{3,2,1,0:T(8,128)(2,1)S(1)}, u32[]{:S(2)}, u32[]{:S(2)}) %collective-permute-start) | collective-permute-done | bytes 589856 | tf_op jit(solution)/shard_map/ppermute | solution.py:165
  6.8 0.1 split_core.1
  7.0 2.9 %collective-permute-start.1 = (bf16[4,24,768]{2,1,0:T(8,128)(2,1)S(1)}, bf16[4,24,768]{2,1,0:T(8,128)(2,1)S(1)}, u32[]{:S(2)}, u32[]{:S(2)}) collective-permute-start(bf16[4,24,768]{2,1,0:T(8,128)(2,1)S(1)} %get-tuple-element.21), channel_id=1, source_target_pairs={{0,2},{1,3},{2,0},{3,1},{4,6},{5,7},{6,4},{7,5},{8,10},{9,11},{10,... | collective-permute-start | bytes 442376 | tf_op jit(solution)/shard_map/ppermute | solution.py:165
  9.9 1.5 %collective-permute-start.2 = (bf16[4,24,768]{2,1,0:T(8,128)(2,1)S(1)}, bf16[4,24,768]{2,1,0:T(8,128)(2,1)S(1)}, u32[]{:S(2)}, u32[]{:S(2)}) collective-permute-start(bf16[4,24,768]{2,1,0:T(8,128)(2,1)S(1)} %get-tuple-element.22), channel_id=1, source_target_pairs={{0,16},{1,17},{2,18},{3,19},{4,20},{5,21},{6,22},{7,23},{8,24},{9,... | collective-permute-start | bytes 442376 | tf_op jit(solution)/shard_map/ppermute | solution.py:165
  11.4 0.0 collective-permute-start.3
  11.4 2.6 %collective-permute-done.1.refs_0_ = bf16[4,24,768]{2,1,0:T(8,128)(2,1)S(1)} collective-permute-done((bf16[4,24,768]{2,1,0:T(8,128)(2,1)S(1)}, bf16[4,24,768]{2,1,0:T(8,128)(2,1)S(1)}, u32[]{:S(2)}, u32[]{:S(2)}) %collective-permute-start.1) | collective-permute-done | bytes 147488 | tf_op jit(solution)/shard_map/ppermute | solution.py:165
  14.0 2.6 %collective-permute-done.2.refs_1_ = bf16[4,24,768]{2,1,0:T(8,128)(2,1)S(1)} collective-permute-done((bf16[4,24,768]{2,1,0:T(8,128)(2,1)S(1)}, bf16[4,24,768]{2,1,0:T(8,128)(2,1)S(1)}, u32[]{:S(2)}, u32[]{:S(2)}) %collective-permute-start.2) | collective-permute-done | bytes 147488 | tf_op jit(solution)/shard_map/ppermute | solution.py:165
  16.6 1.8 %collective-permute-done.3.refs_2_ = bf16[4,24,768]{2,1,0:T(8,128)(2,1)S(1)} collective-permute-done((bf16[4,24,768]{2,1,0:T(8,128)(2,1)S(1)}, bf16[4,24,768]{2,1,0:T(8,128)(2,1)S(1)}, u32[]{:S(2)}, u32[]{:S(2)}) %collective-permute-start.3) | collective-permute-done | bytes 147488 | tf_op jit(solution)/shard_map/ppermute | solution.py:165
  18.5 0.1 split_plane.1
  18.5 1.8 %collective-permute-start.4 = (bf16[24,768]{1,0:T(8,128)(2,1)S(1)}, bf16[24,768]{1,0:T(8,128)(2,1)S(1)}, u32[]{:S(2)}, u32[]{:S(2)}) collective-permute-start(bf16[24,768]{1,0:T(8,128)(2,1)S(1)} %get-tuple-element.25), channel_id=1, source_target_pairs={{0,4},{1,5},{2,6},{3,7},{4,0},{5,1},{6,2},{7,3},{8,12},{9,13},{10,... | collective-permute-start | bytes 110600 | tf_op jit(solution)/shard_map/ppermute | solution.py:165
  20.3 2.6 %collective-permute-start.5 = (bf16[24,768]{1,0:T(8,128)(2,1)S(1)}, bf16[24,768]{1,0:T(8,128)(2,1)S(1)}, u32[]{:S(2)}, u32[]{:S(2)}) collective-permute-start(bf16[24,768]{1,0:T(8,128)(2,1)S(1)} %get-tuple-element.26), channel_id=1, source_target_pairs={{0,8},{1,9},{2,10},{3,11},{4,12},{5,13},{6,14},{7,15},{8,0},{9,1},... | collective-permute-start | bytes 110600 | tf_op jit(solution)/shard_map/ppermute | solution.py:165
  22.9 0.1 collective-permute-start.6
  23.0 0.0 collective-permute-done.4.refs_0_
  23.0 2.5 %collective-permute-done.5.refs_1_ = bf16[24,768]{1,0:T(8,128)(2,1)S(1)} collective-permute-done((bf16[24,768]{1,0:T(8,128)(2,1)S(1)}, bf16[24,768]{1,0:T(8,128)(2,1)S(1)}, u32[]{:S(2)}, u32[]{:S(2)}) %collective-permute-start.5) | collective-permute-done | bytes 36896 | tf_op jit(solution)/shard_map/ppermute | solution.py:165
  25.5 3.2 %collective-permute-done.6.refs_2_ = bf16[24,768]{1,0:T(8,128)(2,1)S(1)} collective-permute-done((bf16[24,768]{1,0:T(8,128)(2,1)S(1)}, bf16[24,768]{1,0:T(8,128)(2,1)S(1)}, u32[]{:S(2)}, u32[]{:S(2)}) %collective-permute-start.6) | collective-permute-done | bytes 36896 | tf_op jit(solution)/shard_map/ppermute | solution.py:165
  28.7 1.7 %adam.1 = (f32[144,128]{1,0:T(8,128)}, f32[144,128]{1,0:T(8,128)}, f32[144,128]{1,0:T(8,128)}, bf16[24,768]{1,0:T(8,128)(2,1)S(1)}) custom-call(f32[24,768]{1,0:T(8,128)S(1)} %get-tuple-element.24.kept, bf16[24,768]{1,0:T(8,128)(2,1)S(1)} %collective-permute-done.4.refs_0_, bf16[24,768]{1,0:T(8,128)(2,1)S(1)} %collective-permute-done.5.refs_1_, ...), custom_call_target="tpu_custom_call" | custom-call | tf_op jit(solution)/shard_map/adam/pallas_call | solution.py:182
  30.4 0.4 collective-permute-start.9
  30.7 0.0 collective-permute-start.8
  30.7 4.0 %collective-permute-start.7 = (bf16[24,768]{1,0:T(8,128)(2,1)S(1)}, bf16[24,768]{1,0:T(8,128)(2,1)S(1)}, u32[]{:S(2)}, u32[]{:S(2)}) collective-permute-start(bf16[24,768]{1,0:T(8,128)(2,1)S(1)} %get-tuple-element.31.refs_0_), channel_id=1, source_target_pairs={{0,4},{1,5},{2,6},{3,7},{4,0},{5,1},{6,2},{7,3},{8,12},{9,13},{10,... | collective-permute-start | bytes 110600 | tf_op jit(solution)/shard_map/ppermute | solution.py:165
  34.8 1.4 %collective-permute-done.9.refs_3_ = bf16[24,768]{1,0:T(8,128)(2,1)S(1)} collective-permute-done((bf16[24,768]{1,0:T(8,128)(2,1)S(1)}, bf16[24,768]{1,0:T(8,128)(2,1)S(1)}, u32[]{:S(2)}, u32[]{:S(2)}) %collective-permute-start.9) | collective-permute-done | bytes 36896 | tf_op jit(solution)/shard_map/ppermute | solution.py:165
  36.1 0.0 collective-permute-done.8.refs_2_
  36.1 0.6 %collective-permute-done.7.refs_1_ = bf16[24,768]{1,0:T(8,128)(2,1)S(1)} collective-permute-done((bf16[24,768]{1,0:T(8,128)(2,1)S(1)}, bf16[24,768]{1,0:T(8,128)(2,1)S(1)}, u32[]{:S(2)}, u32[]{:S(2)}) %collective-permute-start.7) | collective-permute-done | bytes 36896 | tf_op jit(solution)/shard_map/ppermute | solution.py:165
  36.7 10.3 %all-gather = bf16[16,24,768]{2,1,0:T(8,128)(2,1)S(1)} all-gather(bf16[4,24,768]{2,1,0:T(8,128)(2,1)S(1)} %stack_line.1), channel_id=2, replica_groups=mesh['gx'=2,'gy'=4,'gr'=2,'gc'=2] {'gx','gr'}, dimensions={0}, use_global_device_ids=true | all-gather | bytes 737280 | tf_op jit(solution)/shard_map/all_gather | solution.py:197
  47.0 0.0 collective-permute-start.10
  47.0 2.0 %collective-permute-done.10.other = bf16[4,4,24,768]{3,2,1,0:T(8,128)(2,1)S(1)} collective-permute-done((bf16[4,4,24,768]{3,2,1,0:T(8,128)(2,1)S(1)}, bf16[4,4,24,768]{3,2,1,0:T(8,128)(2,1)S(1)}, u32[]{:S(2)}, u32[]{:S(2)}) %collective-permute-start.10) | collective-permute-done | bytes 589856 | tf_op jit(solution)/shard_map/ppermute | solution.py:165
  49.0 1.0 %place.1 = bf16[768,768]{1,0:T(8,128)(2,1)} custom-call(bf16[4,4,24,768]{3,2,1,0:T(8,128)(2,1)S(1)} %bitcast.2, bf16[4,4,24,768]{3,2,1,0:T(8,128)(2,1)S(1)} %collective-permute-done.10.other), custom_call_target="tpu_custom_call" | custom-call | tf_op jit(solution)/shard_map/place/pallas_call | solution.py:198
  (1 shorter events, 0.0 us)
Async XLA Ops:
  4.6 2.2 %collective-permute-start = (bf16[4,4,24,768]{3,2,1,0:T(8,128)(2,1)S(1)}, bf16[4,4,24,768]{3,2,1,0:T(8,128)(2,1)S(1)}, u32[]{:S(2)}, u32[]{:S(2)}) collective-permute-start(bf16[4,4,24,768]{3,2,1,0:T(8,128)(2,1)S(1)} %get-tuple-element.19), channel_id=1, source_target_pairs={{0,1},{1,0},{2,3},{3,2},{4,5},{5,4},{6,7},{7,6},{8,9},{9,8},{10,11... | collective-permute-start | bytes 1769480 | tf_op jit(solution)/shard_map/ppermute | solution.py:165
  7.0 7.1 %collective-permute-start.1 = (bf16[4,24,768]{2,1,0:T(8,128)(2,1)S(1)}, bf16[4,24,768]{2,1,0:T(8,128)(2,1)S(1)}, u32[]{:S(2)}, u32[]{:S(2)}) collective-permute-start(bf16[4,24,768]{2,1,0:T(8,128)(2,1)S(1)} %get-tuple-element.21), channel_id=1, source_target_pairs={{0,2},{1,3},{2,0},{3,1},{4,6},{5,7},{6,4},{7,5},{8,10},{9,11},{10,... | collective-permute-start | bytes 442376 | tf_op jit(solution)/shard_map/ppermute | solution.py:165
  9.9 6.7 %collective-permute-start.2 = (bf16[4,24,768]{2,1,0:T(8,128)(2,1)S(1)}, bf16[4,24,768]{2,1,0:T(8,128)(2,1)S(1)}, u32[]{:S(2)}, u32[]{:S(2)}) collective-permute-start(bf16[4,24,768]{2,1,0:T(8,128)(2,1)S(1)} %get-tuple-element.22), channel_id=1, source_target_pairs={{0,16},{1,17},{2,18},{3,19},{4,20},{5,21},{6,22},{7,23},{8,24},{9,... | collective-permute-start | bytes 442376 | tf_op jit(solution)/shard_map/ppermute | solution.py:165
  11.4 7.1 %collective-permute-start.3 = (bf16[4,24,768]{2,1,0:T(8,128)(2,1)S(1)}, bf16[4,24,768]{2,1,0:T(8,128)(2,1)S(1)}, u32[]{:S(2)}, u32[]{:S(2)}) collective-permute-start(bf16[4,24,768]{2,1,0:T(8,128)(2,1)S(1)} %get-tuple-element.23), channel_id=1, source_target_pairs={{0,18},{1,19},{2,16},{3,17},{4,22},{5,23},{6,20},{7,21},{8,26},{9,... | collective-permute-start | bytes 442376 | tf_op jit(solution)/shard_map/ppermute | solution.py:165
  18.5 4.5 %collective-permute-start.4 = (bf16[24,768]{1,0:T(8,128)(2,1)S(1)}, bf16[24,768]{1,0:T(8,128)(2,1)S(1)}, u32[]{:S(2)}, u32[]{:S(2)}) collective-permute-start(bf16[24,768]{1,0:T(8,128)(2,1)S(1)} %get-tuple-element.25), channel_id=1, source_target_pairs={{0,4},{1,5},{2,6},{3,7},{4,0},{5,1},{6,2},{7,3},{8,12},{9,13},{10,... | collective-permute-start | bytes 110600 | tf_op jit(solution)/shard_map/ppermute | solution.py:165
  20.3 5.2 %collective-permute-start.5 = (bf16[24,768]{1,0:T(8,128)(2,1)S(1)}, bf16[24,768]{1,0:T(8,128)(2,1)S(1)}, u32[]{:S(2)}, u32[]{:S(2)}) collective-permute-start(bf16[24,768]{1,0:T(8,128)(2,1)S(1)} %get-tuple-element.26), channel_id=1, source_target_pairs={{0,8},{1,9},{2,10},{3,11},{4,12},{5,13},{6,14},{7,15},{8,0},{9,1},... | collective-permute-start | bytes 110600 | tf_op jit(solution)/shard_map/ppermute | solution.py:165
  22.9 5.8 %collective-permute-start.6 = (bf16[24,768]{1,0:T(8,128)(2,1)S(1)}, bf16[24,768]{1,0:T(8,128)(2,1)S(1)}, u32[]{:S(2)}, u32[]{:S(2)}) collective-permute-start(bf16[24,768]{1,0:T(8,128)(2,1)S(1)} %get-tuple-element.27), channel_id=1, source_target_pairs={{0,12},{1,13},{2,14},{3,15},{4,8},{5,9},{6,10},{7,11},{8,4},{9,5},... | collective-permute-start | bytes 110600 | tf_op jit(solution)/shard_map/ppermute | solution.py:165
  30.4 5.8 %collective-permute-start.9 = (bf16[24,768]{1,0:T(8,128)(2,1)S(1)}, bf16[24,768]{1,0:T(8,128)(2,1)S(1)}, u32[]{:S(2)}, u32[]{:S(2)}) collective-permute-start(bf16[24,768]{1,0:T(8,128)(2,1)S(1)} %get-tuple-element.31.refs_0_), channel_id=1, source_target_pairs={{0,12},{1,13},{2,14},{3,15},{4,8},{5,9},{6,10},{7,11},{8,4},{9,5},... | collective-permute-start | bytes 110600 | tf_op jit(solution)/shard_map/ppermute | solution.py:165
  30.7 5.4 %collective-permute-start.8 = (bf16[24,768]{1,0:T(8,128)(2,1)S(1)}, bf16[24,768]{1,0:T(8,128)(2,1)S(1)}, u32[]{:S(2)}, u32[]{:S(2)}) collective-permute-start(bf16[24,768]{1,0:T(8,128)(2,1)S(1)} %get-tuple-element.31.refs_0_), channel_id=1, source_target_pairs={{0,8},{1,9},{2,10},{3,11},{4,12},{5,13},{6,14},{7,15},{8,0},{9,1},... | collective-permute-start | bytes 110600 | tf_op jit(solution)/shard_map/ppermute | solution.py:165
  30.7 5.9 %collective-permute-start.7 = (bf16[24,768]{1,0:T(8,128)(2,1)S(1)}, bf16[24,768]{1,0:T(8,128)(2,1)S(1)}, u32[]{:S(2)}, u32[]{:S(2)}) collective-permute-start(bf16[24,768]{1,0:T(8,128)(2,1)S(1)} %get-tuple-element.31.refs_0_), channel_id=1, source_target_pairs={{0,4},{1,5},{2,6},{3,7},{4,0},{5,1},{6,2},{7,3},{8,12},{9,13},{10,... | collective-permute-start | bytes 110600 | tf_op jit(solution)/shard_map/ppermute | solution.py:165
  47.0 2.0 %collective-permute-start.10 = (bf16[4,4,24,768]{3,2,1,0:T(8,128)(2,1)S(1)}, bf16[4,4,24,768]{3,2,1,0:T(8,128)(2,1)S(1)}, u32[]{:S(2)}, u32[]{:S(2)}) collective-permute-start(bf16[4,4,24,768]{3,2,1,0:T(8,128)(2,1)S(1)} %bitcast.1), channel_id=1, source_target_pairs={{0,1},{1,0},{2,3},{3,2},{4,5},{5,4},{6,7},{7,6},{8,9},{9,8},{10,11... | collective-permute-start | bytes 1769480 | tf_op jit(solution)/shard_map/ppermute | solution.py:165
